TPU v7x, 32 devices: a whole 2x2x4 slice. The times are simulated.
32 devices in a mesh: walker: 8 (over z, core), chol: 4 (over y, x).
Axes of the slice: x: 2, y: 2, z: 4, core: 2. Of those that a mesh axis runs over, the one named last changes fastest.
Arguments:
- chol_vectors: bfloat16 [256, 768, 192], P('chol', 'walker'), may hold values from -0.2 to 0.2, as said below
- green: bfloat16 [16, 768, 192], P('walker'), may hold values from -6 to 6
Outputs:
- energy: float32 [16], P('walker')
- gradient: float32 [16, 768, 192], P('walker', 'chol')
Inputs may be any that keep to these rules, and one draw needn't show every extreme that they name: `chol_vectors`: independent entries of each vector; vector magnitudes differ from vector to vector.
All inputs are finite; a program needn't handle non-finite values.
Results may differ from a plain program's by a relative error of at most 0.0042.
Values may be sent and summed in bfloat16 or wider, within the bound.
A program may use at most 128 MiB of HBM per device.

v0:
```python
import jax
import jax.numpy as jnp
from jax import lax
from jax.sharding import PartitionSpec as P

NCHOL = 256


def per_device(chol_vectors, green):
    width = green.shape[2]
    escale = 1.0 / (NCHOL * width)
    gscale = 1.0 / NCHOL**0.5
    tmat = jnp.einsum(
        "kmi,wmj->wkij",
        lax.all_gather(chol_vectors, "walker", axis=1, tiled=True),
        green,
        preferred_element_type=jnp.float32,
    )
    partial_energy = jnp.sum(tmat * jnp.swapaxes(tmat, 2, 3), axis=(1, 2, 3)) * escale
    energy = lax.psum(partial_energy, "chol")
    tround = tmat.astype(jnp.bfloat16)
    terms = jnp.einsum(
        "kmi,wkji->wmj",
        lax.all_gather(chol_vectors, "walker", axis=1, tiled=True),
        tround,
        preferred_element_type=jnp.float32,
    )
    gradient = lax.psum_scatter(terms, "chol", scatter_dimension=1, tiled=True) * gscale
    return (energy, gradient)


def solution(mesh):
    placed = (P("chol", "walker", None), P("walker", None, None))
    return jax.shard_map(
        per_device,
        mesh=mesh,
        in_specs=placed,
        out_specs=(P("walker"), P("walker", "chol", None)),
        check_vma=False,
    )
```

profile of v0, /device:TPU:24, one launch (start us, length us, event | category | flops | bytes accessed | tf_op | source)
XLA Modules:
  0.0 336.8 jit_solution(9373367045362210709)
XLA Ops:
  7.2 0.0 copy-start
  7.2 0.0 all-gather.2.cloned.1.call-start
  7.2 0.7 all-gather.2.cloned.1.call-update
  7.9 0.0 reduce-scatter.4.cloned.1.call-start
  8.0 219.4 %all-gather.2.cloned.1.call-done = bf16[64,768,192]{2,1,0:T(8,128)(2,1)} async-done(((bf16[64,96,192]{2,1,0:T(8,128)(2,1)}), bf16[64,768,192]{2,1,0:T(8,128)(2,1)}) %all-gather.2.cloned.1.call-update) | async-done | bytes 18874384 | tf_op jit(solution)/shard_map/all_gather | solution.py:15
  227.4 0.0 copy-done
  227.4 22.0 %fusion.3 = f32[2,192,64,192]{3,1,2,0:T(8,128)} fusion(bf16[64,768,192]{2,1,0:T(8,128)(2,1)} %all-gather.2.cloned.1.call-done, bf16[2,768,192]{1,2,0:T(8,128)(2,1)S(1)} %copy-done), kind=kOutput, calls=%fused_computation.5 | convolution fusion | flops 7247757312 | bytes 38338560 | tf_op jit(solution)/shard_map/kmi,wmj->wkij/dot_general | solution.py:13
  249.4 25.7 %copy.6 = f32[2,192,64,192]{1,3,2,0:T(8,128)} copy(f32[2,192,64,192]{3,1,2,0:T(8,128)} %fusion.3) | data formatting | bytes 37748736 | tf_op jit(solution)/shard_map/kmi,wmj->wkij/dot_general | solution.py:13
  275.1 19.1 %fusion.5 = f32[2,768,192]{1,2,0:T(8,128)S(1)} fusion(bf16[64,768,192]{2,1,0:T(8,128)(2,1)} %all-gather.2.cloned.1.call-done, f32[2,192,64,192]{1,3,2,0:T(8,128)} %copy.6), kind=kOutput, calls=%fused_computation.7 | convolution fusion | flops 7247757312 | bytes 38928384 | tf_op jit(solution)/shard_map/kmi,wkji->wmj/dot_general | solution.py:22
  294.2 0.8 copy.10
  295.1 2.3 reshape.7
  297.3 0.0 reduce-scatter.4.cloned.1.call-update
  297.3 0.0 copy-start.1
  297.4 17.4 %fusion = f32[2]{0:T(128)S(1)} fusion(f32[2,192,64,192]{3,1,2,0:T(8,128)} %fusion.3, f32[2,192,64,192]{1,3,2,0:T(8,128)} %copy.6), kind=kLoop, calls=%fused_computation.1 | loop fusion | flops 9437182 | bytes 37748744 | tf_op jit(solution)/shard_map/reduce_sum | solution.py:19
  314.8 10.6 %psum.7 = f32[2]{0:T(128)} all-reduce(f32[2]{0:T(128)S(1)} %broadcast_multiply_fusion.1), channel_id=1, replica_groups=mesh['walker'=8,'chol'=4] {'chol'}, use_global_device_ids=true, to_apply=%region_1.0 | all-reduce | flops 2 | bytes 16 | tf_op jit(solution)/shard_map/psum | solution.py:20
  325.4 2.1 reduce-scatter.4.cloned.1.call-done
  327.5 1.2 reshape.8
  328.8 0.2 copy.11
  329.0 0.9 copy.7
  329.9 0.0 copy-done.1
  (2 shorter events, 0.0 us)
Async XLA Ops:
  7.2 220.2 %copy-start = (bf16[2,768,192]{1,2,0:T(8,128)(2,1)S(1)}, bf16[2,768,192]{1,2,0:T(8,128)(2,1)}, u32[]{:S(2)}) copy-start(bf16[2,768,192]{1,2,0:T(8,128)(2,1)} %param.3) | copy-start | bytes 1769476
  7.2 220.2 %all-gather.2.cloned.1.call-start = ((), (), s32[]{:S(2)}) async-start(), calls=%async_computation.1 | async-start | bytes 28311552 | tf_op jit(solution)/shard_map/all_gather | solution.py:15
  7.9 319.6 %reduce-scatter.4.cloned.1.call-start = ((), (), s32[]{:S(2)}) async-start(), calls=%async_computation.2 | async-start | bytes 1474560
  297.3 32.6 %copy-start.1 = (bf16[2,768,192]{1,2,0:T(8,128)(2,1)S(1)}, bf16[2,768,192]{1,2,0:T(8,128)(2,1)}, u32[]{:S(2)}) copy-start(bf16[2,768,192]{1,2,0:T(8,128)(2,1)} %param.3) | copy-start | bytes 1769476
Sparse Core Ops, SparseCore 0:
  9.6 217.7 all-gather.1
  297.5 30.0 reduce-scatter.3
where the time goes:
time: 340 us; the launch traced here: 337 us
  waiting for transfers between devices  222 us (65%)
  matrix products  41.1 us (12%)
  local copies, waits for them, and re-layouts  31.2 us (9%)
  other arithmetic  17.5 us (5%)
  between operations  14.1 us (4%)
  blocking collectives  10.6 us (3%)
    all_gather x1, waiting for transfers between devices, per_device(): lax.all_gather(chol_vectors, 'walker', axis=1, tiled=True)  219 us
    dot_general x1, local copies, waits for them, and re-layouts, per_device(): jnp.einsum('kmi,wmj->wkij', lax.all_gather(chol_vectors, 'walker', axis=1...  25.7 us
    dot_general x1, matrix products, per_device(): jnp.einsum('kmi,wmj->wkij', lax.all_gather(chol_vectors, 'walker', axis=1...  22 us
    dot_general x1, matrix products, per_device(): jnp.einsum('kmi,wkji->wmj', lax.all_gather(chol_vectors, 'walker', axis=1...  19.1 us
    reduce_sum x1, other arithmetic, per_device(): jnp.sum(tmat * jnp.swapaxes(tmat, 2, 3), axis=(1, 2, 3)) * escale  17.4 us
    psum x1, blocking collectives, per_device(): energy = lax.psum(partial_energy, 'chol')  10.6 us
  transfers between devices with their start and end apart: 2, of which 2 were waited for; matrix products, arithmetic and copies ran while one was open for 5% of the time, Pallas kernels for 0%

commit v1 on v0

v1 whole, which is shorter than its diff:
```python
import functools
import math

import jax
import jax.numpy as jnp
from jax import lax
from jax.experimental import pallas as pl
from jax.experimental.pallas import tpu as pltpu
from jax.sharding import PartitionSpec as P

MESH = pl.DeviceIdType.MESH
CORES = 2
ANY = pl.BlockSpec(memory_space=pl.ANY)


def remote(src, dst, send, recv, device):
    return pltpu.make_async_remote_copy(
        src_ref=src, dst_ref=dst, send_sem=send, recv_sem=recv, device_id=device, device_id_type=MESH
    )


def greet(devices):
    barrier = pltpu.get_barrier_semaphore()
    for device in devices:
        pl.semaphore_signal(barrier, inc=1, device_id=device, device_id_type=MESH)
    pl.semaphore_wait(barrier, len(devices))


def gather_kernel(
    span, groups, chol, green, blocks, greens, own_chol, own_green,
    chol_send, chol_recv, pair_send, pair_recv, green_send, green_recv, share_send, share_recv, local,
):
    walker, group = lax.axis_index("walker"), lax.axis_index("chol")
    chip, core = walker // CORES, walker % CORES
    kept, width = blocks.shape[1], green.shape[1] // groups
    partner = (chip * CORES + 1 - core, group)
    peers = [None] + [lax.rem(chip + d, span) for d in range(1, span)]
    sources = [None] + [lax.rem(chip - d + span, span) for d in range(1, span)]
    sides = [None] + [(walker, lax.rem(group + d, groups)) for d in range(1, groups)]
    greet([partner] + [(z * CORES + core, group) for z in peers[1:]] + sides[1:])

    mine = pl.ds(pl.multiple_of(group * width, math.gcd(width, 16)), width)
    waits = []
    first, quarters = [None], [None]
    for d in range(1, span):
        target = (peers[d] * CORES + core, group)
        quarter = remote(
            green.at[:, mine, :], greens.at[chip, :, mine, :], green_send.at[d], green_recv.at[d], target
        )
        quarter.start()
        quarters.append(quarter)
    for d in range(1, span):
        target = (peers[d] * CORES + core, group)
        block = remote(
            chol.at[pl.ds(peers[d] * kept, kept)], blocks.at[walker], chol_send.at[d], chol_recv.at[d], target
        )
        block.start()
        first.append(block)
    held = chol.at[pl.ds(chip * kept, kept)]
    pair = remote(held, blocks.at[walker], pair_send.at[0], pair_recv.at[0], partner)
    pair.start()
    waits.append(pair)
    takes = [pltpu.make_async_copy(held, own_chol, local.at[0]), pltpu.make_async_copy(green, own_green, local.at[1])]
    for take in takes:
        take.start()
    for take in takes:
        take.wait()
    puts = [
        pltpu.make_async_copy(own_chol, blocks.at[walker], local.at[2]),
        pltpu.make_async_copy(own_green, greens.at[chip], local.at[3]),
    ]
    for put in puts:
        put.start()
    for d in range(1, span):
        quarters[d].wait_recv()
        piece = greens.at[sources[d], :, mine, :]
        for e in range(1, groups):
            share = remote(piece, piece, share_send.at[d, e], share_recv.at[d, e], sides[e])
            share.start()
            waits.append(share)
    for d in range(1, span):
        first[d].wait_recv()
        landed = blocks.at[sources[d] * CORES + core]
        pair = remote(landed, landed, pair_send.at[d], pair_recv.at[d], partner)
        pair.start()
        waits.append(pair)
    for put in puts:
        put.wait()
    for d in range(1, span):
        quarters[d].wait_send()
        first[d].wait_send()
    for copy in waits:
        copy.wait()


def gather(span, groups, chol, green):
    kl, mb, width = chol.shape
    wl, m, _ = green.shape
    kept = kl // span
    dma = pltpu.SemaphoreType.DMA
    return pl.pallas_call(
        functools.partial(gather_kernel, span, groups),
        out_shape=(
            jax.ShapeDtypeStruct((span * CORES, kept, mb, width), chol.dtype),
            jax.ShapeDtypeStruct((span, wl, m, width), green.dtype),
        ),
        in_specs=[ANY, ANY],
        out_specs=(ANY, ANY),
        scratch_shapes=[
            pltpu.VMEM((kept, mb, width), chol.dtype),
            pltpu.VMEM((wl, m, width), green.dtype),
            dma((span,)), dma((span,)), dma((span,)), dma((span,)), dma((span,)), dma((span,)),
            dma((span, groups)), dma((span, groups)), dma((4,)),
        ],
        compiler_params=pltpu.CompilerParams(collective_id=0, has_side_effects=True),
    )(chol, green)


def product_kernel(chol, green, terms, energy, turned, total):
    k = pl.program_id(1)
    walkers = green.shape[0]

    @pl.when(k == 0)
    def _():
        total[...] = jnp.zeros_like(total)
        energy[...] = jnp.zeros_like(energy)

    turned[...] = chol[0].T
    per = math.gcd(walkers, 2)

    def step(n, carry):
        for u in range(per):
            w = n * per + u
            tmat = jnp.dot(turned[...], green[w], preferred_element_type=jnp.float32)
            energy[w] += jnp.sum(tmat * tmat.T, axis=0, keepdims=True)
            total[w] += lax.dot_general(
                chol[0], tmat.astype(jnp.bfloat16), (((1,), (1,)), ((), ())), preferred_element_type=jnp.float32
            )
        return carry

    lax.fori_loop(0, walkers // per, step, 0)

    @pl.when(k == pl.num_programs(1) - 1)
    def _():
        terms[...] = total[...].astype(terms.dtype)


def products(chol, green):
    kept, m, width = chol.shape
    walkers = green.shape[0]
    some = math.gcd(walkers, 8)
    return pl.pallas_call(
        product_kernel,
        out_shape=(
            jax.ShapeDtypeStruct((walkers, m, width), jnp.bfloat16),
            jax.ShapeDtypeStruct((walkers, 1, width), jnp.float32),
        ),
        grid=(walkers // some, kept),
        in_specs=[
            pl.BlockSpec((1, m, width), lambda g, k: (k, 0, 0)),
            pl.BlockSpec((some, m, width), lambda g, k: (g, 0, 0)),
        ],
        out_specs=(
            pl.BlockSpec((some, m, width), lambda g, k: (g, 0, 0)),
            pl.BlockSpec((some, 1, width), lambda g, k: (g, 0, 0)),
        ),
        scratch_shapes=[pltpu.VMEM((width, m), jnp.bfloat16), pltpu.VMEM((some, m, width), jnp.float32)],
        compiler_params=pltpu.CompilerParams(
            dimension_semantics=("arbitrary", "arbitrary"), vmem_limit_bytes=60 * 2**20
        ),
    )(chol, green)


def spread_kernel(span, groups, terms, energy, parts, energies, send, recv, esend, erecv):
    walker, group = lax.axis_index("walker"), lax.axis_index("chol")
    chip, core = walker // CORES, walker % CORES
    wl, width = parts.shape[1], parts.shape[2]
    others = [(d, e) for d in range(span) for e in range(groups) if d + e > 0]
    target = {(d, e): (lax.rem(chip + d, span), lax.rem(group + e, groups)) for d, e in others}
    greet([(target[o][0] * CORES + core, target[o][1]) for o in others])
    copies = []
    for n, o in enumerate(others):
        z, q = target[o]
        device = (z * CORES + core, q)
        block = terms.at[pl.ds(z * wl, wl), pl.ds(pl.multiple_of(q * width, math.gcd(width, 16)), width), :]
        copies.append(remote(block, parts.at[n], send.at[n], recv.at[n], device))
        copies.append(remote(energy.at[z], energies.at[n], esend.at[n], erecv.at[n], device))
    for copy in copies:
        copy.start()
    for copy in copies:
        copy.wait()


def spread(span, groups, terms, energy):
    walkers, m, width = terms.shape
    count = span * groups - 1
    dma = pltpu.SemaphoreType.DMA
    return pl.pallas_call(
        functools.partial(spread_kernel, span, groups),
        out_shape=(
            jax.ShapeDtypeStruct((count, walkers // span, m // groups, width), terms.dtype),
            jax.ShapeDtypeStruct((count,) + energy.shape[1:], energy.dtype),
        ),
        in_specs=[ANY, ANY],
        out_specs=(ANY, ANY),
        scratch_shapes=[dma((count,)), dma((count,)), dma((count,)), dma((count,))],
        compiler_params=pltpu.CompilerParams(collective_id=1, has_side_effects=True),
    )(terms, energy)


def per_device(span, groups, chol_vectors, green):
    kl, mb, width = chol_vectors.shape
    wl, m, _ = green.shape
    nchol = kl * groups
    escale = 1.0 / (nchol * width)
    gscale = 1.0 / nchol**0.5
    chip, group = lax.axis_index("walker") // CORES, lax.axis_index("chol")

    blocks, greens = gather(span, groups, chol_vectors, green)
    chol = jnp.transpose(blocks, (1, 0, 2, 3)).reshape(kl // span, m, width)
    terms, lines = products(chol, greens.reshape(span * wl, m, width))

    sums = jnp.sum(lines, axis=(1, 2)).reshape(span, wl, 1)
    sums = jnp.broadcast_to(sums, (span, wl, 128))
    parts, energies = spread(span, groups, terms, sums)
    own = lax.dynamic_slice(terms, (chip * wl, group * (m // groups), 0), (wl, m // groups, width))
    gradient = (own.astype(jnp.float32) + jnp.sum(parts.astype(jnp.float32), axis=0)) * gscale
    energy = lax.dynamic_index_in_dim(sums, chip, 0, keepdims=False) + jnp.sum(energies, axis=0)
    return energy[:, 0] * escale, gradient


def solution(mesh):
    span, groups = mesh.shape["walker"] // CORES, mesh.shape["chol"]
    return jax.shard_map(
        functools.partial(per_device, span, groups),
        mesh=mesh,
        in_specs=(P("chol", "walker", None), P("walker", None, None)),
        out_specs=(P("walker"), P("walker", "chol", None)),
        check_vma=False,
    )
```

time: 340 us -> 253 us (0.74)
  Pallas kernels: 0 us -> 237 us
  waiting for transfers between devices: 222 us -> 0 us
  matrix products: 41.1 us -> 0 us
  local copies, waits for them, and re-layouts: 31.2 us -> 9.06 us
  between operations: 14.1 us -> 0.68 us
  other arithmetic: 17.5 us -> 6.37 us
  blocking collectives: 10.6 us -> 0 us
    pallas_call x0 -> x3, Pallas kernels: none -> 237 us  [the longest x1 91.9 us: gather(): pl.pallas_call(functools.partial(gather_kernel, span, groups), out_shape=...]
    all_gather x1 -> x0, waiting for transfers between devices: 219 us -> none  [per_device(): lax.all_gather(chol_vectors, 'walker', axis=1, tiled=True)]
    dot_general x2 -> x0, matrix products: 41.1 us -> none  [the longest x1 22 us: per_device(): jnp.einsum('kmi,wmj->wkij', lax.all_gather(chol_vectors, 'walker', axis=1...]
    dot_general x1 -> x0, local copies, waits for them, and re-layouts: 25.7 us -> none  [per_device(): jnp.einsum('kmi,wmj->wkij', lax.all_gather(chol_vectors, 'walker', axis=1...]
    reduce_sum x1 -> x3, other arithmetic: 17.4 us -> 3.94 us  [the longest x1 2.36 us: per_device(): jnp.sum(parts.astype(jnp.float32), axis=0)]
    psum x1 -> x0, blocking collectives: 10.6 us -> none  [per_device(): energy = lax.psum(partial_energy, 'chol')]
    transpose x0 -> x1, local copies, waits for them, and re-layouts: none -> 6.07 us  [per_device(): chol = jnp.transpose(blocks, (1, 0, 2, 3)).reshape(kl // span, m, width)]
  transfers between devices with their start and end apart: 2 -> 0, of which waited for: 2 -> 0; matrix products, arithmetic and copies ran while one was open for 5% -> 0% of each run, Pallas kernels for 0% -> 0%
where the time goes in v1:
time: 253 us
  Pallas kernels  237 us (94%)
  local copies, waits for them, and re-layouts  9.06 us (4%)
  other arithmetic  6.37 us (3%)
    pallas_call x1, Pallas kernels, gather(): pl.pallas_call(functools.partial(gather_kernel, span, groups), out_shape=...  91.9 us
    pallas_call x1, Pallas kernels, spread(): pl.pallas_call(functools.partial(spread_kernel, span, groups), out_shape=...  76.3 us
    pallas_call x1, Pallas kernels, products(): pl.pallas_call(product_kernel, out_shape=(jax.ShapeDtypeStruct((walkers,...  68.5 us
    transpose x1, local copies, waits for them, and re-layouts, per_device(): chol = jnp.transpose(blocks, (1, 0, 2, 3)).reshape(kl // span, m, width)  6.07 us

profile of v1, /device:TPU:24, one launch (start us, length us, event | category | flops | bytes accessed | tf_op | source)
XLA Modules:
  0.0 252.8 jit_solution(12355399944224627747)
XLA Ops:
  0.6 2.2 copy.10.green
  2.9 91.9 %shard_map.41 = (bf16[8,16,96,192]{3,2,1,0:T(8,128)(2,1)}, bf16[4,2,768,192]{3,2,1,0:T(8,128)(2,1)}) custom-call(bf16[64,96,192]{2,1,0:T(8,128)(2,1)} %chol.1, bf16[2,768,192]{2,1,0:T(8,128)(2,1)} %copy.10.green), custom_call_target="tpu_custom_call" | custom-call | tf_op jit(solution)/shard_map/pallas_call | solution.py:101
  94.7 6.1 %copy.11 = bf16[16,8,96,192]{3,2,1,0:T(8,128)(2,1)} copy(bf16[16,8,96,192]{3,2,0,1:T(8,128)(2,1)} %bitcast.6) | data formatting | bytes 9437184 | tf_op jit(solution)/shard_map/transpose | solution.py:220
  100.8 68.5 %shard_map.42 = (bf16[8,768,192]{2,1,0:T(8,128)(2,1)}, f32[8,1,192]{2,1,0:T(1,128)}) custom-call(bf16[16,768,192]{2,1,0:T(8,128)(2,1)} %bitcast.5, bf16[8,768,192]{2,1,0:T(8,128)(2,1)} %bitcast.7), custom_call_target="tpu_custom_call" | custom-call | tf_op jit(solution)/shard_map/pallas_call | solution.py:152
  169.3 0.8 reduce_sum.27
  170.2 0.1 broadcast_in_dim.11
  170.2 0.7 broadcast_in_dim.14.energy
  170.9 76.3 %shard_map.43 = (bf16[15,2,192,192]{3,2,1,0:T(8,128)(2,1)}, f32[15,2,128]{2,1,0:T(2,128)}) custom-call(bf16[8,768,192]{2,1,0:T(8,128)(2,1)} %get-tuple-element.11.terms, f32[4,2,128]{2,1,0:T(2,128)} %broadcast_in_dim.14.energy), custom_call_target="tpu_custom_call" | custom-call | tf_op jit(solution)/shard_map/pallas_call | solution.py:198
  247.2 0.7 reduce_sum.28
  248.0 0.1 broadcast_add_fusion
  248.0 0.6 multiply_reduce_fusion
  248.7 2.4 convert_reduce_fusion
  251.0 1.7 add_multiply_fusion
  (1 shorter events, 0.0 us)

commit v2 on v1

--- a/solution.py
+++ b/solution.py
@@ -126,7 +126,7 @@
         energy[...] = jnp.zeros_like(energy)
 
     turned[...] = chol[0].T
-    per = math.gcd(walkers, 2)
+    per = math.gcd(walkers, 4)
 
     def step(n, carry):
         for u in range(per):

time: 253 us -> 228 us (0.901)
  Pallas kernels: 237 us -> 212 us
    pallas_call x1, Pallas kernels: 68.5 us -> 43.5 us  [products(): pl.pallas_call(product_kernel, out_shape=(jax.ShapeDtypeStruct((walkers,...]
where the time goes in v2:
time: 228 us
  Pallas kernels  212 us (93%)
  local copies, waits for them, and re-layouts  9.06 us (4%)
  other arithmetic  6.37 us (3%)
    pallas_call x1, Pallas kernels, gather(): pl.pallas_call(functools.partial(gather_kernel, span, groups), out_shape=...  91.9 us
    pallas_call x1, Pallas kernels, spread(): pl.pallas_call(functools.partial(spread_kernel, span, groups), out_shape=...  76.3 us
    pallas_call x1, Pallas kernels, products(): pl.pallas_call(product_kernel, out_shape=(jax.ShapeDtypeStruct((walkers,...  43.5 us
    transpose x1, local copies, waits for them, and re-layouts, per_device(): chol = jnp.transpose(blocks, (1, 0, 2, 3)).reshape(kl // span, m, width)  6.07 us

profile of v2, /device:TPU:24, one launch (start us, length us, event | category | flops | bytes accessed | tf_op | source)
XLA Modules:
  0.0 227.7 jit_solution(3528654978375088735)
XLA Ops:
  0.6 2.2 copy.10.green
  2.9 91.9 %shard_map.41 = (bf16[8,16,96,192]{3,2,1,0:T(8,128)(2,1)}, bf16[4,2,768,192]{3,2,1,0:T(8,128)(2,1)}) custom-call(bf16[64,96,192]{2,1,0:T(8,128)(2,1)} %chol.1, bf16[2,768,192]{2,1,0:T(8,128)(2,1)} %copy.10.green), custom_call_target="tpu_custom_call" | custom-call | tf_op jit(solution)/shard_map/pallas_call | solution.py:101
  94.7 6.1 %copy.11 = bf16[16,8,96,192]{3,2,1,0:T(8,128)(2,1)} copy(bf16[16,8,96,192]{3,2,0,1:T(8,128)(2,1)} %bitcast.6) | data formatting | bytes 9437184 | tf_op jit(solution)/shard_map/transpose | solution.py:220
  100.8 43.5 %shard_map.42 = (bf16[8,768,192]{2,1,0:T(8,128)(2,1)}, f32[8,1,192]{2,1,0:T(1,128)}) custom-call(bf16[16,768,192]{2,1,0:T(8,128)(2,1)} %bitcast.5, bf16[8,768,192]{2,1,0:T(8,128)(2,1)} %bitcast.7), custom_call_target="tpu_custom_call" | custom-call | tf_op jit(solution)/shard_map/pallas_call | solution.py:152
  144.3 0.8 reduce_sum.27
  145.1 0.1 broadcast_in_dim.11
  145.2 0.7 broadcast_in_dim.14.energy
  145.9 76.3 %shard_map.43 = (bf16[15,2,192,192]{3,2,1,0:T(8,128)(2,1)}, f32[15,2,128]{2,1,0:T(2,128)}) custom-call(bf16[8,768,192]{2,1,0:T(8,128)(2,1)} %get-tuple-element.11.terms, f32[4,2,128]{2,1,0:T(2,128)} %broadcast_in_dim.14.energy), custom_call_target="tpu_custom_call" | custom-call | tf_op jit(solution)/shard_map/pallas_call | solution.py:198
  222.1 0.7 reduce_sum.28
  222.9 0.1 broadcast_add_fusion
  223.0 0.6 multiply_reduce_fusion
  223.6 2.4 %convert_reduce_fusion = f32[2,192,192]{2,1,0:T(8,128)S(1)} fusion(bf16[15,2,192,192]{3,2,1,0:T(8,128)(2,1)} %get-tuple-element.13), kind=kLoop, calls=%fused_computation | loop fusion | flops 2138112 | bytes 2506752 | tf_op jit(solution)/shard_map/reduce_sum | solution.py:227
  226.0 1.7 add_multiply_fusion
  (1 shorter events, 0.0 us)
